TPU v7x, 32 devices: a whole 2x2x4 slice. The times are simulated.
32 devices in a mesh: section: 4 (over x, core), head: 8 (over z, y).
Axes of the slice: x: 2, y: 2, z: 4, core: 2. Of those that a mesh axis runs over, the one named last changes fastest.
Arguments:
- hidden: float32 [4, 32, 7168], P(None, 'section'), may hold values from -6 to 6
- norm_gain: float32 [7168], replicated, may hold values from 0.5 to 1.5
- router: bfloat16 [7168, 8], replicated, may hold values from -0.0625 to 0.0625
- key_value_weight: bfloat16 [7168, 256], replicated, may hold values from -0.0625 to 0.0625
- query_master: float32 [7168, 1024], P('section', 'head'), may hold values from -0.0625 to 0.0625
- output_master: float32 [7168, 1024], P('section', 'head'), may hold values from -1 to 1
- key_value_cache: bfloat16 [32, 256, 256], P('section', 'head'), may hold values from -480 to 480
- lengths: int32 [32], P('section'), may hold values from 64 to 256
- routes: int32 [4, 32, 4], P(None, 'section'), may hold values from 0 to 7, all different within a row
Outputs:
- handed_on: float32 [4, 32, 7168], P(None, 'section', 'head')
All inputs are finite; a program needn't handle non-finite values.
Results may differ from a plain program's by a relative error of at most 0.012.
The roundings to bfloat16 on the way count: a program that leaves them out, or rounds other values in their place, can miss the bound.
Values may be sent and summed in bfloat16 or wider, within the bound.
No kernel may reach another device: no remote copies, remote signals or barrier semaphores. Data moves between devices by JAX's collectives and lax.ppermute only.
A program may use at most 64 MiB of HBM per device.

v0:
```python
import math
import jax
import jax.numpy as jnp
from jax import lax
from jax.sharding import PartitionSpec as P


def from_behind(value, axis, steps):
    count = lax.axis_size(axis)
    pairs = [(source, (source + steps) % count) for source in range(count)]
    return lax.ppermute(value, axis, pairs)


def body(
    hidden,
    norm_gain,
    router,
    key_value_weight,
    query_master,
    output_master,
    key_value_cache,
    lengths,
    routes,
):
    step_count, row_count, model_width = hidden.shape
    head_dim = key_value_weight.shape[1] // 2
    experts = router.shape[1]
    own_expert = lax.axis_index("head")
    query_piece = query_master.astype(jnp.bfloat16)
    output_piece = output_master.astype(jnp.bfloat16)
    query_weight, output_weight = (
        lax.all_gather(query_piece, "section", axis=0, tiled=True),
        lax.all_gather(output_piece, "section", axis=0, tiled=True),
    )
    mean_square = jnp.mean(hidden * hidden, axis=-1, keepdims=True)
    normed = (hidden * lax.rsqrt(mean_square + 1e-05) * norm_gain).astype(jnp.bfloat16)
    flat_rows = normed.reshape(step_count * row_count, model_width)
    logits = jnp.dot(flat_rows, router, preferred_element_type=jnp.float32).reshape(
        step_count, row_count, experts
    )
    expert_ids = jnp.arange(experts)
    chosen = jnp.sum((routes[..., None] == expert_ids).astype(jnp.float32), axis=2)
    picked = jax.nn.sigmoid(logits) * chosen
    gate_values = picked / jnp.sum(picked, axis=-1, keepdims=True)
    fresh_pairs = jnp.dot(flat_rows, key_value_weight, preferred_element_type=jnp.float32).astype(
        jnp.bfloat16
    )
    fresh_pairs = fresh_pairs.reshape(step_count, row_count, 2 * head_dim)
    key_new = fresh_pairs[..., :head_dim]
    value_new = fresh_pairs[..., head_dim:]
    queries = jnp.dot(flat_rows, query_weight, preferred_element_type=jnp.float32).astype(
        jnp.bfloat16
    )
    queries = queries.reshape(step_count, row_count, head_dim)
    score_factor = 1.0 / math.sqrt(head_dim)
    step_order = jnp.arange(step_count)
    fresh_mask = (step_order[None, :] <= step_order[:, None])[:, None, :]
    fresh_scores = (
        jnp.einsum("srh,urh->sru", queries, key_new, preferred_element_type=jnp.float32)
        * score_factor
    )
    fresh_peak = jnp.max(jnp.where(fresh_mask, fresh_scores, -jnp.inf), axis=-1)
    gathered = lax.all_gather(key_value_cache, "head", axis=1, tiled=True)
    positions = jnp.arange(gathered.shape[1])
    cache_mask = (positions[None, :] < lengths[:, None])[None, :, :]
    cache_scores = (
        jnp.einsum(
            "srh,rph->srp", queries, gathered[..., :head_dim], preferred_element_type=jnp.float32
        )
        * score_factor
    )
    highest = jnp.maximum(
        jnp.max(jnp.where(cache_mask, cache_scores, -jnp.inf), axis=-1), fresh_peak
    )
    cache_weights = jnp.where(cache_mask, jnp.exp(cache_scores - highest[..., None]), 0.0)
    mixture = jnp.einsum(
        "srp,rph->srh", cache_weights, gathered[..., head_dim:], preferred_element_type=jnp.float32
    )
    denominator = jnp.sum(cache_weights, axis=-1)
    fresh_weights = jnp.where(fresh_mask, jnp.exp(fresh_scores - highest[..., None]), 0.0)
    mixture = mixture + jnp.einsum(
        "sru,urh->srh", fresh_weights, value_new, preferred_element_type=jnp.float32
    )
    denominator = denominator + jnp.sum(fresh_weights, axis=-1)
    attended = (mixture / denominator[..., None]).astype(jnp.bfloat16)
    share_width = model_width // lax.axis_size("head")
    feature_slice = lax.all_to_all(output_weight, "head", split_axis=0, concat_axis=1, tiled=True)
    feature_slice = feature_slice.reshape(share_width, experts, head_dim)
    all_attended = lax.all_gather(attended[:, :, None, :], "head", axis=2, tiled=True)
    all_attended = all_attended.reshape(step_count * row_count, experts, head_dim)
    per_expert = jnp.einsum(
        "neh,feh->nef", all_attended, feature_slice, preferred_element_type=jnp.float32
    )
    gates_flat = gate_values.reshape(step_count * row_count, experts)
    summed = jnp.sum(gates_flat[..., None] * per_expert, axis=1)
    summed = summed.reshape(step_count, row_count, share_width)
    own_columns = lax.dynamic_slice_in_dim(hidden, own_expert * share_width, share_width, 2)
    result = own_columns + summed
    return from_behind(result, "section", 1)


def solution(mesh):
    return jax.shard_map(
        body,
        mesh=mesh,
        in_specs=(
            P(None, "section", None),
            P(),
            P(),
            P(),
            P("section", "head"),
            P("section", "head"),
            P("section", "head", None),
            P("section"),
            P(None, "section", None),
        ),
        out_specs=P(None, "section", "head"),
        check_vma=False,
    )
```

profile of v0, /device:TPU:0, one launch (start us, length us, event | category | flops | bytes accessed | tf_op | source)
XLA Modules:
  0.0 139.1 jit_solution(11316484669414816470)
XLA Ops:
  6.5 0.0 copy-start
  6.5 0.0 copy-start.2
  6.5 0.0 copy-start.1
  6.5 0.0 all-gather.9.cloned.1.call-start
  6.5 2.1 %convert_element_type.27 = bf16[1792,128]{1,0:T(8,128)(2,1)} convert(f32[1792,128]{1,0:T(8,128)} %param.14) | non-fusion elementwise | flops 229376 | bytes 1376256 | tf_op jit(solution)/shard_map/convert_element_type | solution.py:30
  8.7 0.0 all-gather.9.cloned.1.call-update
  8.7 0.0 all-gather.5.cloned.1.call-start
  8.8 0.0 copy-done.2
  8.8 0.8 convert_element_type.23
  9.6 0.0 all-gather.5.cloned.1.call-update
  9.6 0.0 all-gather.7.cloned.1.call-start
  9.7 0.7 all-gather.7.cloned.1.call-update
  10.3 0.0 copy-done.1
  10.4 0.2 multiply_reduce_fusion
  10.5 22.2 %all-gather.9.cloned.1.call-done = bf16[7168,128]{1,0:T(8,128)(2,1)} async-done(((bf16[1792,128]{1,0:T(8,128)(2,1)}), bf16[7168,128]{1,0:T(8,128)(2,1)}) %all-gather.9.cloned.1.call-update) | async-done | bytes 1835024 | tf_op jit(solution)/shard_map/all_gather | solution.py:33
  32.7 0.0 copy-start.3
  32.8 0.0 copy-start.4
  32.8 5.6 %all-to-all-start = ((bf16[8,896,128]{2,1,0:T(8,128)(2,1)}), bf16[8,896,128]{2,1,0:T(8,128)(2,1)S(1)}, u32[]{:S(2)}, u32[]{:S(2)}) async-start(bf16[8,896,128]{2,1,0:T(8,128)(2,1)} %bitcast.56), calls=%async_computation | async-start | bytes 3670016 | tf_op jit(solution)/shard_map/all_to_all | solution.py:87
  38.4 0.0 copy-done.3
  38.4 0.0 copy-start.5
  38.4 0.2 multiply_convert_fusion
  38.6 0.0 copy-done.4
  38.6 0.1 convert_reduce_fusion
  38.7 0.1 copy.25
  38.8 0.0 copy-done
  38.8 1.1 fusion.43
  39.9 0.1 mul.60
  40.0 0.0 copy-done.5
  40.0 0.1 iota_compare_fusion.1
  40.1 3.0 %fusion.12 = bf16[4,8,256]{2,1,0:T(8,128)(2,1)S(1)} fusion(bf16[7168,256]{1,0:T(8,128)(2,1)} %param.12, bf16[4,8,7168]{2,1,0:T(8,128)(2,1)S(1)} %multiply_convert_fusion), kind=kOutput, calls=%fused_computation.8 | convolution fusion | flops 117448704 | bytes 4145152 | tf_op jit(solution)/shard_map/dot_general | solution.py:45
  43.1 12.3 %all-gather.5.cloned.1.call-done = bf16[7168,128]{1,0:T(8,128)(2,1)} async-done(((bf16[1792,128]{1,0:T(8,128)(2,1)}), bf16[7168,128]{1,0:T(8,128)(2,1)}) %all-gather.5.cloned.1.call-update) | async-done | bytes 1835024 | tf_op jit(solution)/shard_map/all_gather | solution.py:32
  55.4 1.9 %fusion.21 = bf16[4,8,128]{2,1,0:T(8,128)(2,1)S(1)} fusion(bf16[7168,128]{1,0:T(8,128)(2,1)} %all-gather.5.cloned.1.call-done, bf16[4,8,7168]{2,1,0:T(8,128)(2,1)S(1)} %multiply_convert_fusion), kind=kOutput, calls=%fused_computation.22 | convolution fusion | flops 58724352 | bytes 2301952 | tf_op jit(solution)/shard_map/dot_general | solution.py:51
  57.3 0.1 select_reduce_fusion.1
  57.5 47.6 %all-gather.7.cloned.1.call-done = bf16[8,256,256]{2,1,0:T(8,128)(2,1)} async-done(((bf16[8,32,256]{2,1,0:T(8,128)(2,1)}), bf16[8,256,256]{2,1,0:T(8,128)(2,1)}) %all-gather.7.cloned.1.call-update) | async-done | bytes 1048592 | tf_op jit(solution)/shard_map/all_gather | solution.py:63
  105.1 1.4 select_reduce_fusion
  106.5 0.2 fusion.28
  106.7 1.3 convolution_bitcast_fusion.1
  108.0 0.2 fusion.20
  108.2 18.6 %all-gather = bf16[4,8,1024]{2,0,1:T(4,128)(2,1)S(1)} all-gather(bf16[4,8,128]{2,0,1:T(4,128)(2,1)S(1)} %fusion.20), channel_id=2, replica_groups=mesh['section'=4,'head'=8] {'head'}, dimensions={2}, use_global_device_ids=true | all-gather | bytes 73728 | tf_op jit(solution)/shard_map/all_gather | solution.py:89
  126.9 0.0 all-to-all-done
  126.9 0.7 fusion.8
  127.6 0.1 collective-permute-start
  127.7 4.2 %collective-permute-done = f32[4,8,896]{2,1,0:T(8,128)S(1)} collective-permute-done((f32[4,8,896]{2,1,0:T(8,128)S(1)}, f32[4,8,896]{2,1,0:T(8,128)S(1)}, u32[]{:S(2)}, u32[]{:S(2)}) %collective-permute-start) | collective-permute-done | bytes 114720 | tf_op jit(solution)/shard_map/ppermute | solution.py:11
  131.9 0.6 copy.57
  (11 shorter events, 0.1 us)
Async XLA Ops:
  6.5 32.2 %copy-start = (bf16[7168,8]{0,1:T(8,128)(2,1)S(1)}, bf16[7168,8]{0,1:T(8,128)(2,1)}, u32[]{:S(2)}) copy-start(bf16[7168,8]{0,1:T(8,128)(2,1)} %param.11) | copy-start | bytes 344068
  6.5 2.2 %copy-start.2 = (f32[1792,128]{1,0:T(8,128)S(1)}, f32[1792,128]{1,0:T(8,128)}, u32[]{:S(2)}) copy-start(f32[1792,128]{1,0:T(8,128)} %param.13) | copy-start | bytes 2752516
  6.5 3.8 %copy-start.1 = (f32[4,8,7168]{2,1,0:T(8,128)S(1)}, f32[4,8,7168]{2,1,0:T(8,128)}, u32[]{:S(2)}) copy-start(f32[4,8,7168]{2,1,0:T(8,128)} %param.9) | copy-start | bytes 2752516
  6.5 26.2 %all-gather.9.cloned.1.call-start = ((), (), s32[]{:S(2)}) async-start(), calls=%async_computation.3 | async-start | bytes 2293760 | tf_op jit(solution)/shard_map/all_gather | solution.py:33
  8.7 46.7 %all-gather.5.cloned.1.call-start = ((), (), s32[]{:S(2)}) async-start(), calls=%async_computation.1 | async-start | bytes 2293760 | tf_op jit(solution)/shard_map/all_gather | solution.py:32
  9.6 95.5 %all-gather.7.cloned.1.call-start = ((), (), s32[]{:S(2)}) async-start(), calls=%async_computation.2 | async-start | bytes 1179648 | tf_op jit(solution)/shard_map/all_gather | solution.py:63
  32.7 5.7 %copy-start.3 = (f32[7168]{0:T(1024)S(1)}, f32[7168]{0:T(1024)}, u32[]{:S(2)}) copy-start(f32[7168]{0:T(1024)} %param.10) | copy-start | bytes 86020
  32.8 5.8 %copy-start.4 = (s32[4,8,4]{1,2,0:T(4,128)S(1)}, s32[4,8,4]{1,2,0:T(4,128)}, u32[]{:S(2)}) copy-start(s32[4,8,4]{1,2,0:T(4,128)} %param.17) | copy-start | bytes 1540
  32.8 94.1 %all-to-all-start = ((bf16[8,896,128]{2,1,0:T(8,128)(2,1)}), bf16[8,896,128]{2,1,0:T(8,128)(2,1)S(1)}, u32[]{:S(2)}, u32[]{:S(2)}) async-start(bf16[8,896,128]{2,1,0:T(8,128)(2,1)} %bitcast.56), calls=%async_computation | async-start | bytes 3670016 | tf_op jit(solution)/shard_map/all_to_all | solution.py:87
  38.4 1.6 %copy-start.5 = (s32[8]{0:T(128)S(1)}, s32[8]{0:T(128)}, u32[]{:S(2)}) copy-start(s32[8]{0:T(128)} %param.16) | copy-start | bytes 100
  127.6 4.3 %collective-permute-start = (f32[4,8,896]{2,1,0:T(8,128)S(1)}, f32[4,8,896]{2,1,0:T(8,128)S(1)}, u32[]{:S(2)}, u32[]{:S(2)}) collective-permute-start(f32[4,8,896]{2,1,0:T(8,128)S(1)} %bitcast_add_fusion), channel_id=1, source_target_pairs={{0,8},{8,16},{16,24},{24,0},{1,9},{9,17},{17,25},{25,1},{2,10},{10... | collective-permute-start | bytes 344072 | tf_op jit(solution)/shard_map/ppermute | solution.py:11
Sparse Core Ops, SparseCore 0:
  8.9 23.8 all-gather.8
  34.3 21.0 all-gather.4
  57.6 47.4 all-gather.6
where the time goes:
time: 140 us; the launch traced here: 139 us
  waiting for transfers between devices  87.1 us (62%)
  blocking collectives  18.6 us (13%)
  between operations  13.3 us (10%)
  matrix products  9.74 us (7%)
  starting transfers between devices  5.79 us (4%)
  other arithmetic  3.71 us (3%)
    all_gather x1, waiting for transfers between devices, body(): gathered = lax.all_gather(key_value_cache, 'head', axis=1, tiled=True)  47.6 us
    all_gather x1, waiting for transfers between devices, body(): lax.all_gather(output_piece, 'section', axis=0, tiled=True)  22.2 us
    all_gather x1, blocking collectives, body(): lax.all_gather(attended[:, :, None, :], 'head', axis=2, tiled=True)  18.6 us
    all_gather x1, waiting for transfers between devices, body(): lax.all_gather(query_piece, 'section', axis=0, tiled=True)  12.3 us
    all_to_all x1, starting transfers between devices, body(): lax.all_to_all(output_weight, 'head', split_axis=0, concat_axis=1, tiled=...  5.65 us
    ppermute x1, waiting for transfers between devices, from_behind(): return lax.ppermute(value, axis, pairs)  4.2 us
    dot_general x1, matrix products, body(): jnp.dot(flat_rows, key_value_weight, preferred_element_type=jnp.float32)  2.97 us
  transfers between devices with their start and end apart: 5, of which 4 were waited for; matrix products, arithmetic and copies ran while one was open for 8% of the time, Pallas kernels for 0%

commit v1 on v0

--- a/solution.py
+++ b/solution.py
@@ -60,7 +60,12 @@
         * score_factor
     )
     fresh_peak = jnp.max(jnp.where(fresh_mask, fresh_scores, -jnp.inf), axis=-1)
-    gathered = lax.all_gather(key_value_cache, "head", axis=1, tiled=True)
+    ring = [key_value_cache]
+    for hop in range(7):
+        ring.append(lax.ppermute(ring[-1], "head", [(dev, (dev + 1) % 8) for dev in range(8)]))
+    gathered = jnp.roll(
+        jnp.concatenate(ring[::-1], axis=1), (lax.axis_index("head") + 1) * ring[0].shape[1], axis=1
+    )
     positions = jnp.arange(gathered.shape[1])
     cache_mask = (positions[None, :] < lengths[:, None])[None, :, :]
     cache_scores = (

time: 140 us -> 124 us (0.89)
  waiting for transfers between devices: 87.1 us -> 47.9 us
  local copies, waits for them, and re-layouts: 0.87 us -> 20.4 us
  starting transfers between devices: 5.79 us -> 9.33 us
    all_gather x1 -> x0, waiting for transfers between devices: 47.6 us -> none  [body(): gathered = lax.all_gather(key_value_cache, 'head', axis=1, tiled=True)]
    ppermute x0 -> x7, waiting for transfers between devices: none -> 43.7 us  [body(): lax.ppermute(ring[-1], 'head', [(dev, (dev + 1) % 8) for dev in range(8)])]
    all_gather x1, waiting for transfers between devices: 22.2 us -> 0.01 us  [body(): lax.all_gather(output_piece, 'section', axis=0, tiled=True)]
    unnamed x14 -> x51, local copies, waits for them, and re-layouts: 0.68 us -> 19.6 us
    all_gather x1, waiting for transfers between devices: 12.3 us -> 0.01 us  [body(): lax.all_gather(query_piece, 'section', axis=0, tiled=True)]
    ppermute x0 -> x7, starting transfers between devices: none -> 3.06 us  [body(): lax.ppermute(ring[-1], 'head', [(dev, (dev + 1) % 8) for dev in range(8)])]
  transfers between devices with their start and end apart: 5 -> 11, of which waited for: 4 -> 8; matrix products, arithmetic and copies ran while one was open for 8% -> 24% of each run, Pallas kernels for 0% -> 0%
where the time goes in v1:
time: 124 us; the launch traced here: 123 us
  waiting for transfers between devices  47.9 us (39%)
  local copies, waits for them, and re-layouts  20.4 us (16%)
  blocking collectives  18.5 us (15%)
  between operations  13.6 us (11%)
  matrix products  9.6 us (8%)
  starting transfers between devices  9.33 us (8%)
  other arithmetic  3.68 us (3%)
    ppermute x7, waiting for transfers between devices, body(): lax.ppermute(ring[-1], 'head', [(dev, (dev + 1) % 8) for dev in range(8)])  43.7 us
    unnamed x51, local copies, waits for them, and re-layouts  19.6 us
    all_gather x1, blocking collectives, body(): lax.all_gather(attended[:, :, None, :], 'head', axis=2, tiled=True)  18.5 us
    all_to_all x1, starting transfers between devices, body(): lax.all_to_all(output_weight, 'head', split_axis=0, concat_axis=1, tiled=...  6.14 us
    ppermute x1, waiting for transfers between devices, from_behind(): return lax.ppermute(value, axis, pairs)  4.2 us
    ppermute x7, starting transfers between devices, body(): lax.ppermute(ring[-1], 'head', [(dev, (dev + 1) % 8) for dev in range(8)])  3.06 us
    dot_general x1, matrix products, body(): jnp.dot(flat_rows, key_value_weight, preferred_element_type=jnp.float32)  2.83 us
  transfers between devices with their start and end apart: 11, of which 8 were waited for; matrix products, arithmetic and copies ran while one was open for 24% of the time, Pallas kernels for 0%

profile of v1, /device:TPU:0, one launch (start us, length us, event | category | flops | bytes accessed | tf_op | source)
XLA Modules:
  0.0 123.1 jit_solution(9709237775303472976)
XLA Ops:
  6.5 0.0 all-gather.6.cloned.1.call-start
  6.6 2.1 %convert_element_type.27 = bf16[1792,128]{1,0:T(8,128)(2,1)} convert(f32[1792,128]{1,0:T(8,128)} %param.14) | non-fusion elementwise | flops 229376 | bytes 1376256 | tf_op jit(solution)/shard_map/convert_element_type | solution.py:30
  8.7 0.0 all-gather.6.cloned.1.call-update
  8.7 0.0 all-gather.4.cloned.1.call-start
  8.8 3.0 %collective-permute-start = (bf16[8,32,256]{2,1,0:T(8,128)(2,1)}, bf16[8,32,256]{2,1,0:T(8,128)(2,1)S(1)}, u32[]{:S(2)}, u32[]{:S(2)}) collective-permute-start(bf16[8,32,256]{2,1,0:T(8,128)(2,1)} %param.15), channel_id=1, source_target_pairs={{0,1},{1,2},{2,3},{3,4},{4,5},{5,6},{6,7},{7,0},{8,9},{9,10},{10,1... | collective-permute-start | bytes 393224 | tf_op jit(solution)/shard_map/ppermute | solution.py:65
  11.8 0.8 convert_element_type.23
  12.7 0.0 all-gather.4.cloned.1.call-update
  12.7 0.2 multiply_reduce_fusion
  12.9 5.7 %collective-permute-done = bf16[8,32,256]{2,1,0:T(8,128)(2,1)S(1)} collective-permute-done((bf16[8,32,256]{2,1,0:T(8,128)(2,1)}, bf16[8,32,256]{2,1,0:T(8,128)(2,1)S(1)}, u32[]{:S(2)}, u32[]{:S(2)}) %collective-permute-start) | collective-permute-done | bytes 131104 | tf_op jit(solution)/shard_map/ppermute | solution.py:65
  18.6 0.0 collective-permute-start.1
  18.6 0.0 copy-done.14
  18.6 0.2 multiply_convert_fusion
  18.8 0.0 copy-start.15
  18.8 0.0 copy-start.16
  18.8 7.5 %collective-permute-done.1 = bf16[8,32,256]{2,1,0:T(8,128)(2,1)S(1)} collective-permute-done((bf16[8,32,256]{2,1,0:T(8,128)(2,1)S(1)}, bf16[8,32,256]{2,1,0:T(8,128)(2,1)S(1)}, u32[]{:S(2)}, u32[]{:S(2)}) %collective-permute-start.1) | collective-permute-done | bytes 131104 | tf_op jit(solution)/shard_map/ppermute | solution.py:65
  26.3 0.0 collective-permute-start.2
  26.3 2.8 %fusion.12 = bf16[4,8,256]{2,1,0:T(8,128)(2,1)S(1)} fusion(bf16[7168,256]{1,0:T(8,128)(2,1)} %param.12, bf16[4,8,7168]{2,1,0:T(8,128)(2,1)S(1)} %multiply_convert_fusion), kind=kOutput, calls=%fused_computation.8 | convolution fusion | flops 117448704 | bytes 4145152 | tf_op jit(solution)/shard_map/dot_general | solution.py:45
  29.1 0.0 copy-done.4
  29.1 0.1 convert_reduce_fusion
  29.2 0.1 copy.25
  29.3 4.6 %collective-permute-done.2 = bf16[8,32,256]{2,1,0:T(8,128)(2,1)S(1)} collective-permute-done((bf16[8,32,256]{2,1,0:T(8,128)(2,1)S(1)}, bf16[8,32,256]{2,1,0:T(8,128)(2,1)S(1)}, u32[]{:S(2)}, u32[]{:S(2)}) %collective-permute-start.2) | collective-permute-done | bytes 131104 | tf_op jit(solution)/shard_map/ppermute | solution.py:65
  33.9 0.0 collective-permute-start.3
  33.9 1.1 fusion.46
  35.1 6.5 %collective-permute-done.3 = bf16[8,32,256]{2,1,0:T(8,128)(2,1)S(1)} collective-permute-done((bf16[8,32,256]{2,1,0:T(8,128)(2,1)S(1)}, bf16[8,32,256]{2,1,0:T(8,128)(2,1)S(1)}, u32[]{:S(2)}, u32[]{:S(2)}) %collective-permute-start.3) | collective-permute-done | bytes 131104 | tf_op jit(solution)/shard_map/ppermute | solution.py:65
  41.6 0.0 collective-permute-start.4
  41.6 7.7 %collective-permute-done.4 = bf16[8,32,256]{2,1,0:T(8,128)(2,1)S(1)} collective-permute-done((bf16[8,32,256]{2,1,0:T(8,128)(2,1)S(1)}, bf16[8,32,256]{2,1,0:T(8,128)(2,1)S(1)}, u32[]{:S(2)}, u32[]{:S(2)}) %collective-permute-start.4) | collective-permute-done | bytes 131104 | tf_op jit(solution)/shard_map/ppermute | solution.py:65
  49.3 0.6 copy-done.12
  49.9 0.0 collective-permute-start.5
  49.9 8.6 %collective-permute-done.5 = bf16[8,32,256]{2,1,0:T(8,128)(2,1)} collective-permute-done((bf16[8,32,256]{2,1,0:T(8,128)(2,1)S(1)}, bf16[8,32,256]{2,1,0:T(8,128)(2,1)}, u32[]{:S(2)}, u32[]{:S(2)}) %collective-permute-start.5) | collective-permute-done | bytes 131104 | tf_op jit(solution)/shard_map/ppermute | solution.py:65
  58.6 0.0 collective-permute-start.6
  58.6 0.0 copy-done.16
  58.6 0.1 iota_compare_fusion.1
  58.6 0.1 mul.63
  58.7 0.0 copy-done.8
  58.8 6.1 %all-to-all-start = ((bf16[8,896,128]{2,1,0:T(8,128)(2,1)}), bf16[8,896,128]{2,1,0:T(8,128)(2,1)S(1)}, u32[]{:S(2)}, u32[]{:S(2)}) async-start(bf16[8,896,128]{2,1,0:T(8,128)(2,1)} %bitcast.52), calls=%async_computation | async-start | bytes 3670016 | tf_op jit(solution)/shard_map/all_to_all | solution.py:92
  64.9 3.1 %collective-permute-done.6 = bf16[8,32,256]{2,1,0:T(8,128)(2,1)} collective-permute-done((bf16[8,32,256]{2,1,0:T(8,128)(2,1)}, bf16[8,32,256]{2,1,0:T(8,128)(2,1)}, u32[]{:S(2)}, u32[]{:S(2)}) %collective-permute-start.6) | collective-permute-done | bytes 131104 | tf_op jit(solution)/shard_map/ppermute | solution.py:65
  68.0 1.6 %constant_dynamic-update-slice_fusion.15 = bf16[8,512,256]{2,1,0:T(8,128)(2,1)} fusion(bf16[8,32,256]{2,1,0:T(8,128)(2,1)} %collective-permute-done.6), kind=kLoop, calls=%fused_computation.49 | loop fusion | bytes 262144
  69.6 1.6 %constant_dynamic-update-slice_fusion.14 = bf16[8,512,256]{2,1,0:T(8,128)(2,1)} fusion(bf16[8,512,256]{2,1,0:T(8,128)(2,1)} %constant_dynamic-update-slice_fusion.15, bf16[8,32,256]{2,1,0:T(8,128)(2,1)} %collective-permute-done.5), kind=kLoop, calls=%fused_computation.48 | loop fusion | bytes 262144
  71.2 1.6 %constant_dynamic-update-slice_fusion.13 = bf16[8,512,256]{2,1,0:T(8,128)(2,1)} fusion(bf16[8,512,256]{2,1,0:T(8,128)(2,1)} %constant_dynamic-update-slice_fusion.14, bf16[8,32,256]{2,1,0:T(8,128)(2,1)} %copy-done.12), kind=kLoop, calls=%fused_computation.47 | loop fusion | bytes 262144
  72.7 1.6 %constant_dynamic-update-slice_fusion.12 = bf16[8,512,256]{2,1,0:T(8,128)(2,1)} fusion(bf16[8,512,256]{2,1,0:T(8,128)(2,1)} %constant_dynamic-update-slice_fusion.13, bf16[8,32,256]{2,1,0:T(8,128)(2,1)} %copy-done.10), kind=kLoop, calls=%fused_computation.46 | loop fusion | bytes 262144
  74.3 1.6 %constant_dynamic-update-slice_fusion.11 = bf16[8,512,256]{2,1,0:T(8,128)(2,1)} fusion(bf16[8,512,256]{2,1,0:T(8,128)(2,1)} %constant_dynamic-update-slice_fusion.12, bf16[8,32,256]{2,1,0:T(8,128)(2,1)} %copy-done.8), kind=kLoop, calls=%fused_computation.45 | loop fusion | bytes 262144
  75.9 1.6 %constant_dynamic-update-slice_fusion.10 = bf16[8,512,256]{2,1,0:T(8,128)(2,1)} fusion(bf16[8,512,256]{2,1,0:T(8,128)(2,1)} %constant_dynamic-update-slice_fusion.11, bf16[8,32,256]{2,1,0:T(8,128)(2,1)} %copy-done.6), kind=kLoop, calls=%fused_computation.44 | loop fusion | bytes 262144
  77.4 1.6 %constant_dynamic-update-slice_fusion.9 = bf16[8,512,256]{2,1,0:T(8,128)(2,1)} fusion(bf16[8,512,256]{2,1,0:T(8,128)(2,1)} %constant_dynamic-update-slice_fusion.10, bf16[8,32,256]{2,1,0:T(8,128)(2,1)} %copy-done.4), kind=kLoop, calls=%fused_computation.43 | loop fusion | bytes 262144
  79.0 0.7 constant_dynamic-update-slice_fusion.8
  79.7 1.6 %constant_dynamic-update-slice_fusion.7 = bf16[8,512,256]{2,1,0:T(8,128)(2,1)} fusion(bf16[8,512,256]{2,1,0:T(8,128)(2,1)} %constant_dynamic-update-slice_fusion.8, bf16[8,32,256]{2,1,0:T(8,128)(2,1)} %collective-permute-done.6), kind=kLoop, calls=%fused_computation.41 | loop fusion | bytes 262144
  81.3 1.6 %constant_dynamic-update-slice_fusion.6 = bf16[8,512,256]{2,1,0:T(8,128)(2,1)} fusion(bf16[8,512,256]{2,1,0:T(8,128)(2,1)} %constant_dynamic-update-slice_fusion.7, bf16[8,32,256]{2,1,0:T(8,128)(2,1)} %collective-permute-done.5), kind=kLoop, calls=%fused_computation.40 | loop fusion | bytes 262144
  82.9 0.7 constant_dynamic-update-slice_fusion.5
  83.5 0.7 constant_dynamic-update-slice_fusion.4
  84.2 0.7 constant_dynamic-update-slice_fusion.3
  84.8 0.7 constant_dynamic-update-slice_fusion.2
  85.5 0.7 constant_dynamic-update-slice_fusion.1
  86.2 0.7 constant_dynamic-update-slice_fusion
  86.9 1.9 %fusion.21 = bf16[4,8,128]{2,1,0:T(8,128)(2,1)S(1)} fusion(bf16[7168,128]{1,0:T(8,128)(2,1)} %all-gather.4.cloned.1.call-done, bf16[4,8,7168]{2,1,0:T(8,128)(2,1)S(1)} %multiply_convert_fusion), kind=kOutput, calls=%fused_computation.21 | convolution fusion | flops 58724352 | bytes 2301952 | tf_op jit(solution)/shard_map/dot_general | solution.py:51
  88.8 0.1 select_reduce_fusion.1
  88.9 1.4 %select_reduce_fusion = (f32[4,8]{0,1:T(8,128)S(1)}, f32[4,8,256]{2,0,1:T(4,128)S(1)}) fusion(pred[8,256]{1,0:T(8,128)(4,1)S(1)} %iota_compare_fusion.1, bf16[4,8,128]{2,1,0:T(8,128)(2,1)S(1)} %fusion.21, bf16[8,512,256]{2,1,0:T(8,128)(2,1)} %constant_dynamic-update-slice_fusion, s32[]{:T(128)S(6)} %select_n.32), kind=kOutput, calls=%fused_computation.51 | convolution fusion | flops 2121696 | bytes 567428 | tf_op jit(solution)/shard_map/srh,rph->srp/dot_general | solution.py:72
  90.3 0.2 fusion.28
  90.5 0.2 fusion.33
  90.7 1.3 %fusion.20 = bf16[4,8,128]{2,0,1:T(4,128)(2,1)S(1)} fusion(f32[8,128,4]{1,2,0:T(4,128)S(1)} %fusion.33, bf16[8,512,256]{2,1,0:T(8,128)(2,1)} %constant_dynamic-update-slice_fusion, s32[]{:T(128)S(6)} %select_n.32, s32[]{:T(128)S(6)} %add.57, f32[4,8,256]{2,0,1:T(4,128)S(1)} %get-tuple-element.10, f32[4,8]{0,1:T(8,128)S(1)} %max.7, ...), kind=kOutput, calls=%fused_computation.19 | convolution fusion | flops 2125824 | bytes 583944 | tf_op jit(solution)/shard_map/srp,rph->srh/dot_general | solution.py:81
  92.0 18.5 %all-gather = bf16[4,8,1024]{2,0,1:T(4,128)(2,1)S(1)} all-gather(bf16[4,8,128]{2,0,1:T(4,128)(2,1)S(1)} %fusion.20), channel_id=2, replica_groups=mesh['section'=4,'head'=8] {'head'}, dimensions={2}, use_global_device_ids=true | all-gather | bytes 73728 | tf_op jit(solution)/shard_map/all_gather | solution.py:94
  110.6 0.0 all-to-all-done
  110.6 0.7 fusion.8
  111.4 0.1 collective-permute-start.7
  111.4 4.2 %collective-permute-done.7 = f32[4,8,896]{2,1,0:T(8,128)S(1)} collective-permute-done((f32[4,8,896]{2,1,0:T(8,128)S(1)}, f32[4,8,896]{2,1,0:T(8,128)S(1)}, u32[]{:S(2)}, u32[]{:S(2)}) %collective-permute-start.7) | collective-permute-done | bytes 114720 | tf_op jit(solution)/shard_map/ppermute | solution.py:11
  115.6 0.6 copy.72
  (40 shorter events, 0.2 us)
Async XLA Ops:
  6.5 27.4 %copy-start = (bf16[7168,8]{0,1:T(8,128)(2,1)S(1)}, bf16[7168,8]{0,1:T(8,128)(2,1)}, u32[]{:S(2)}) copy-start(bf16[7168,8]{0,1:T(8,128)(2,1)} %param.11) | copy-start | bytes 344068
  6.5 5.3 %copy-start.2 = (f32[1792,128]{1,0:T(8,128)S(1)}, f32[1792,128]{1,0:T(8,128)}, u32[]{:S(2)}) copy-start(f32[1792,128]{1,0:T(8,128)} %param.13) | copy-start | bytes 2752516
  6.5 6.1 %copy-start.1 = (f32[4,8,7168]{2,1,0:T(8,128)S(1)}, f32[4,8,7168]{2,1,0:T(8,128)}, u32[]{:S(2)}) copy-start(f32[4,8,7168]{2,1,0:T(8,128)} %param.9) | copy-start | bytes 2752516
  6.5 12.1 %copy-start.14 = (f32[7168]{0:T(1024)S(1)}, f32[7168]{0:T(1024)}, u32[]{:S(2)}) copy-start(f32[7168]{0:T(1024)} %param.10) | copy-start | bytes 86020
  6.5 52.2 %all-gather.6.cloned.1.call-start = ((), (), s32[]{:S(2)}) async-start(), calls=%async_computation.2 | async-start | bytes 2293760 | tf_op jit(solution)/shard_map/all_gather | solution.py:33
  8.7 78.1 %all-gather.4.cloned.1.call-start = ((), (), s32[]{:S(2)}) async-start(), calls=%async_computation.1 | async-start | bytes 2293760 | tf_op jit(solution)/shard_map/all_gather | solution.py:32
  8.8 9.8 %collective-permute-start = (bf16[8,32,256]{2,1,0:T(8,128)(2,1)}, bf16[8,32,256]{2,1,0:T(8,128)(2,1)S(1)}, u32[]{:S(2)}, u32[]{:S(2)}) collective-permute-start(bf16[8,32,256]{2,1,0:T(8,128)(2,1)} %param.15), channel_id=1, source_target_pairs={{0,1},{1,2},{2,3},{3,4},{4,5},{5,6},{6,7},{7,0},{8,9},{9,10},{10,1... | collective-permute-start | bytes 393224 | tf_op jit(solution)/shard_map/ppermute | solution.py:65
  18.6 10.5 %copy-start.4 = (bf16[8,32,256]{2,1,0:T(8,128)(2,1)}, bf16[8,32,256]{2,1,0:T(8,128)(2,1)S(1)}, u32[]{:S(2)}) copy-start(bf16[8,32,256]{2,1,0:T(8,128)(2,1)S(1)} %collective-permute-done) | copy-start | bytes 393220
  18.6 7.7 %collective-permute-start.1 = (bf16[8,32,256]{2,1,0:T(8,128)(2,1)S(1)}, bf16[8,32,256]{2,1,0:T(8,128)(2,1)S(1)}, u32[]{:S(2)}, u32[]{:S(2)}) collective-permute-start(bf16[8,32,256]{2,1,0:T(8,128)(2,1)S(1)} %collective-permute-done), channel_id=1, source_target_pairs={{0,1},{1,2},{2,3},{3,4},{4,5},{5,6},{6,7},{7,0},{8,9},{9,10},{10,1... | collective-permute-start | bytes 393224 | tf_op jit(solution)/shard_map/ppermute | solution.py:65
  18.8 10.4 %copy-start.15 = (s32[4,8,4]{1,2,0:T(4,128)S(1)}, s32[4,8,4]{1,2,0:T(4,128)}, u32[]{:S(2)}) copy-start(s32[4,8,4]{1,2,0:T(4,128)} %param.17) | copy-start | bytes 1540
  18.8 39.8 %copy-start.16 = (s32[8]{0:T(128)S(1)}, s32[8]{0:T(128)}, u32[]{:S(2)}) copy-start(s32[8]{0:T(128)} %param.16) | copy-start | bytes 100
  26.3 3.0 %copy-start.6 = (bf16[8,32,256]{2,1,0:T(8,128)(2,1)}, bf16[8,32,256]{2,1,0:T(8,128)(2,1)S(1)}, u32[]{:S(2)}) copy-start(bf16[8,32,256]{2,1,0:T(8,128)(2,1)S(1)} %collective-permute-done.1) | copy-start | bytes 393220
  26.3 7.7 %collective-permute-start.2 = (bf16[8,32,256]{2,1,0:T(8,128)(2,1)S(1)}, bf16[8,32,256]{2,1,0:T(8,128)(2,1)S(1)}, u32[]{:S(2)}, u32[]{:S(2)}) collective-permute-start(bf16[8,32,256]{2,1,0:T(8,128)(2,1)S(1)} %collective-permute-done.1), channel_id=1, source_target_pairs={{0,1},{1,2},{2,3},{3,4},{4,5},{5,6},{6,7},{7,0},{8,9},{9,10},{10,1... | collective-permute-start | bytes 393224 | tf_op jit(solution)/shard_map/ppermute | solution.py:65
  33.9 24.8 %copy-start.8 = (bf16[8,32,256]{2,1,0:T(8,128)(2,1)}, bf16[8,32,256]{2,1,0:T(8,128)(2,1)S(1)}, u32[]{:S(2)}) copy-start(bf16[8,32,256]{2,1,0:T(8,128)(2,1)S(1)} %collective-permute-done.2) | copy-start | bytes 393220
  33.9 7.7 %collective-permute-start.3 = (bf16[8,32,256]{2,1,0:T(8,128)(2,1)S(1)}, bf16[8,32,256]{2,1,0:T(8,128)(2,1)S(1)}, u32[]{:S(2)}, u32[]{:S(2)}) collective-permute-start(bf16[8,32,256]{2,1,0:T(8,128)(2,1)S(1)} %collective-permute-done.2), channel_id=1, source_target_pairs={{0,1},{1,2},{2,3},{3,4},{4,5},{5,6},{6,7},{7,0},{8,9},{9,10},{10,1... | collective-permute-start | bytes 393224 | tf_op jit(solution)/shard_map/ppermute | solution.py:65
  41.6 17.2 %copy-start.10 = (bf16[8,32,256]{2,1,0:T(8,128)(2,1)}, bf16[8,32,256]{2,1,0:T(8,128)(2,1)S(1)}, u32[]{:S(2)}) copy-start(bf16[8,32,256]{2,1,0:T(8,128)(2,1)S(1)} %collective-permute-done.3) | copy-start | bytes 393220
  41.6 7.7 %collective-permute-start.4 = (bf16[8,32,256]{2,1,0:T(8,128)(2,1)S(1)}, bf16[8,32,256]{2,1,0:T(8,128)(2,1)S(1)}, u32[]{:S(2)}, u32[]{:S(2)}) collective-permute-start(bf16[8,32,256]{2,1,0:T(8,128)(2,1)S(1)} %collective-permute-done.3), channel_id=1, source_target_pairs={{0,1},{1,2},{2,3},{3,4},{4,5},{5,6},{6,7},{7,0},{8,9},{9,10},{10,1... | collective-permute-start | bytes 393224 | tf_op jit(solution)/shard_map/ppermute | solution.py:65
  49.3 0.7 copy-start.12
  49.9 8.6 %collective-permute-start.5 = (bf16[8,32,256]{2,1,0:T(8,128)(2,1)S(1)}, bf16[8,32,256]{2,1,0:T(8,128)(2,1)}, u32[]{:S(2)}, u32[]{:S(2)}) collective-permute-start(bf16[8,32,256]{2,1,0:T(8,128)(2,1)S(1)} %collective-permute-done.4), channel_id=1, source_target_pairs={{0,1},{1,2},{2,3},{3,4},{4,5},{5,6},{6,7},{7,0},{8,9},{9,10},{10,1... | collective-permute-start | bytes 393224 | tf_op jit(solution)/shard_map/ppermute | solution.py:65
  58.6 9.4 %collective-permute-start.6 = (bf16[8,32,256]{2,1,0:T(8,128)(2,1)}, bf16[8,32,256]{2,1,0:T(8,128)(2,1)}, u32[]{:S(2)}, u32[]{:S(2)}) collective-permute-start(bf16[8,32,256]{2,1,0:T(8,128)(2,1)} %collective-permute-done.5), channel_id=1, source_target_pairs={{0,1},{1,2},{2,3},{3,4},{4,5},{5,6},{6,7},{7,0},{8,9},{9,10},{10,1... | collective-permute-start | bytes 393224 | tf_op jit(solution)/shard_map/ppermute | solution.py:65
  58.7 20.3 %copy-start.3 = (bf16[8,32,256]{2,1,0:T(8,128)(2,1)S(1)}, bf16[8,32,256]{2,1,0:T(8,128)(2,1)}, u32[]{:S(2)}) copy-start(bf16[8,32,256]{2,1,0:T(8,128)(2,1)} %param.15) | copy-start | bytes 393220
  58.8 51.8 %all-to-all-start = ((bf16[8,896,128]{2,1,0:T(8,128)(2,1)}), bf16[8,896,128]{2,1,0:T(8,128)(2,1)S(1)}, u32[]{:S(2)}, u32[]{:S(2)}) async-start(bf16[8,896,128]{2,1,0:T(8,128)(2,1)} %bitcast.52), calls=%async_computation | async-start | bytes 3670016 | tf_op jit(solution)/shard_map/all_to_all | solution.py:92
  64.9 17.9 %copy-start.13 = (bf16[8,32,256]{2,1,0:T(8,128)(2,1)S(1)}, bf16[8,32,256]{2,1,0:T(8,128)(2,1)}, u32[]{:S(2)}) copy-start(bf16[8,32,256]{2,1,0:T(8,128)(2,1)} %copy-done.12) | copy-start | bytes 393220
  64.9 18.6 %copy-start.11 = (bf16[8,32,256]{2,1,0:T(8,128)(2,1)S(1)}, bf16[8,32,256]{2,1,0:T(8,128)(2,1)}, u32[]{:S(2)}) copy-start(bf16[8,32,256]{2,1,0:T(8,128)(2,1)} %copy-done.10) | copy-start | bytes 393220
  64.9 19.3 %copy-start.9 = (bf16[8,32,256]{2,1,0:T(8,128)(2,1)S(1)}, bf16[8,32,256]{2,1,0:T(8,128)(2,1)}, u32[]{:S(2)}) copy-start(bf16[8,32,256]{2,1,0:T(8,128)(2,1)} %copy-done.8) | copy-start | bytes 393220
  64.9 19.9 %copy-start.7 = (bf16[8,32,256]{2,1,0:T(8,128)(2,1)S(1)}, bf16[8,32,256]{2,1,0:T(8,128)(2,1)}, u32[]{:S(2)}) copy-start(bf16[8,32,256]{2,1,0:T(8,128)(2,1)} %copy-done.6) | copy-start | bytes 393220
  64.9 20.6 %copy-start.5 = (bf16[8,32,256]{2,1,0:T(8,128)(2,1)S(1)}, bf16[8,32,256]{2,1,0:T(8,128)(2,1)}, u32[]{:S(2)}) copy-start(bf16[8,32,256]{2,1,0:T(8,128)(2,1)} %copy-done.4) | copy-start | bytes 393220
  111.4 4.3 %collective-permute-start.7 = (f32[4,8,896]{2,1,0:T(8,128)S(1)}, f32[4,8,896]{2,1,0:T(8,128)S(1)}, u32[]{:S(2)}, u32[]{:S(2)}) collective-permute-start(f32[4,8,896]{2,1,0:T(8,128)S(1)} %bitcast_add_fusion), channel_id=1, source_target_pairs={{0,8},{8,16},{16,24},{24,0},{1,9},{9,17},{17,25},{25,1},{2,10},{10... | collective-permute-start | bytes 344072 | tf_op jit(solution)/shard_map/ppermute | solution.py:11
Sparse Core Ops, SparseCore 0:
  8.9 23.8 all-gather.5
  34.3 21.0 all-gather.3
